TPU v7x, 32 devices: a whole 2x2x4 slice. The times are simulated.
32 devices in a mesh: dp: 8 (over y, x, core), mp: 4 (over z).
Axes of the slice: x: 2, y: 2, z: 4, core: 2. Of those that a mesh axis runs over, the one named last changes fastest.
Arguments:
- block_input: bfloat16 [192, 196, 512], P('dp'), may hold values from -6 to 6
- out_grad: bfloat16 [192, 196, 512], P('dp'), may hold values from -6 to 6
- norm_gains: bfloat16 [512, 2], P('dp'), may hold values from 0.5 to 1.5
- offsets: bfloat16 [512, 4], P('dp'), may hold values from -3 to 3
- qkv_weight: bfloat16 [512, 3, 512], P('dp', None, 'mp'), may hold values from -2 to 2
- qv_bias: bfloat16 [2, 512], P(None, 'mp'), may hold values from -3 to 3
- pos_table: float32 [16, 169], P('mp'), may hold values from -4 to 4
- proj_weight: bfloat16 [512, 512], P('dp', 'mp'), may hold values from -0.75 to 0.75
- fc1_weight: bfloat16 [512, 2048], P('dp', 'mp'), may hold values from -0.25 to 0.25
- fc1_bias: bfloat16 [2048], P('mp'), may hold values from -3 to 3
- fc2_weight: bfloat16 [512, 2048], P('dp', 'mp'), may hold values from -0.125 to 0.125
- rel_index: int32 [49, 49], replicated, may hold values from 0 to 168
- region_ids: int32 [14, 14], replicated, may hold values from 0 to 3
Outputs:
- block_output: bfloat16 [192, 196, 512], P('dp')
- input_grad: bfloat16 [192, 196, 512], P('dp')
- norm_gains_grad: float32 [512, 2], P('dp')
- offsets_grad: float32 [512, 4], P('dp')
- qkv_weight_grad: float32 [512, 3, 512], P('dp', None, 'mp')
- qv_bias_grad: float32 [2, 512], P(None, 'mp')
- pos_table_grad: float32 [16, 169], P('mp')
- proj_weight_grad: float32 [512, 512], P('dp', 'mp')
- fc1_weight_grad: float32 [512, 2048], P('dp', 'mp')
- fc1_bias_grad: float32 [2048], P('mp')
- fc2_weight_grad: float32 [512, 2048], P('dp', 'mp')
All inputs are finite; a program needn't handle non-finite values.
Results may differ from a plain program's by a relative error of at most 0.04.
The roundings to bfloat16 on the way count: a program that leaves them out, or rounds other values in their place, can miss the bound.
Values may be sent and summed in bfloat16 or wider, within the bound.
A program may use at most 256 MiB of HBM per device.

v0:
```python
import math
import jax
import jax.numpy as jnp
from jax import lax
from jax.sharding import PartitionSpec as P

D = 512
HD = 32
WIN = 7
SHIFT = 3
SIDE = 14
TOK_IMG = 196


def window_order(tokens_in):
    image_count, channels = (tokens_in.shape[0], tokens_in.shape[-1])
    side_wins = SIDE // WIN
    grid_view = jnp.roll(
        tokens_in.reshape(image_count, SIDE, SIDE, channels), (-SHIFT, -SHIFT), axis=(1, 2)
    )
    grid_view = grid_view.reshape(image_count, side_wins, WIN, side_wins, WIN, channels).transpose(
        0, 1, 3, 2, 4, 5
    )
    return grid_view.reshape(image_count, SIDE * SIDE, channels)


def grid_order(tokens_in):
    image_count, channels = (tokens_in.shape[0], tokens_in.shape[-1])
    side_wins = SIDE // WIN
    grid_view = tokens_in.reshape(image_count, side_wins, side_wins, WIN, WIN, channels).transpose(
        0, 1, 3, 2, 4, 5
    )
    grid_view = jnp.roll(
        grid_view.reshape(image_count, SIDE, SIDE, channels), (SHIFT, SHIFT), axis=(1, 2)
    )
    return grid_view.reshape(image_count, SIDE * SIDE, channels)


def layer_norm(values, gain_col, shift_col):
    row_mean = jnp.mean(values, axis=-1, keepdims=True)
    centred = values - row_mean
    variance = jnp.mean(centred * centred, axis=-1, keepdims=True)
    inv_std = lax.rsqrt(variance + 1e-05)
    normed = centred * inv_std
    return (normed, inv_std, normed * gain_col + shift_col)


def norm_back(grad_out, normed, inv_std, gain_col):
    scaled = grad_out * gain_col
    return inv_std * (
        scaled
        - jnp.mean(scaled, axis=-1, keepdims=True)
        - normed * jnp.mean(scaled * normed, axis=-1, keepdims=True)
    )


def gelu_parts(pre_act):
    cdf_val = 0.5 * (1.0 + jax.scipy.special.erf(pre_act * (1.0 / math.sqrt(2.0))))
    density = jnp.exp(-0.5 * pre_act * pre_act) * (1.0 / math.sqrt(2.0 * math.pi))
    return (pre_act * cdf_val, cdf_val + pre_act * density)


def window_terms(table_rows, rel_index, region_ids, block_size):
    table_len = table_rows.shape[1]
    win_pos = rel_index.shape[0]
    one_hot = (
        rel_index.reshape(-1)[:, None] == jnp.arange(table_len, dtype=jnp.int32)[None, :]
    ).astype(jnp.float32)
    pos_bias = jnp.dot(table_rows, one_hot.T, precision=lax.Precision.HIGHEST).reshape(
        -1, win_pos, win_pos
    )
    side_wins = SIDE // WIN
    labels = (
        region_ids.reshape(side_wins, WIN, side_wins, WIN)
        .transpose(0, 2, 1, 3)
        .reshape(side_wins * side_wins, win_pos)
    )
    penalty = jnp.where(labels[:, :, None] == labels[:, None, :], 0.0, -100.0).astype(jnp.float32)
    win_bias = pos_bias[None] + penalty[:, None]
    return (jnp.tile(win_bias, (block_size, 1, 1, 1)), one_hot)


def blocked():
    for block_size in range(12, 0, -1):
        return block_size
    return 1


def along_rows(left_mat, right_mat):
    return lax.dot_general(
        left_mat, right_mat, (((0,), (0,)), ((), ())), preferred_element_type=jnp.float32
    )


def along_cols(left_mat, right_mat):
    return lax.dot_general(
        left_mat, right_mat, (((1,), (1,)), ((), ())), preferred_element_type=jnp.float32
    )


def attend(queries, key_rows, values, win_bias):
    scores = (
        jnp.einsum("bqhc,bkhc->bhqk", queries, key_rows, preferred_element_type=jnp.float32)
        + win_bias
    )
    row_max = jnp.max(scores, axis=-1, keepdims=True)
    weights_raw = jnp.exp(scores - row_max)
    row_total = jnp.sum(weights_raw, axis=-1, keepdims=True)
    probs = (weights_raw / row_total).astype(jnp.bfloat16)
    attn_rows = jnp.einsum(
        "bhqk,bkhc->bqhc", probs, values, preferred_element_type=jnp.float32
    ).astype(jnp.bfloat16)
    return (attn_rows, (row_max + jnp.log(row_total))[..., 0])


def attend_back(queries, key_rows, values, attn_rows, grad_attn, log_total, win_bias, score_scale):
    scores = (
        jnp.einsum("bqhc,bkhc->bhqk", queries, key_rows, preferred_element_type=jnp.float32)
        + win_bias
    )
    probs = jnp.exp(scores - log_total[..., None])
    grad_probs = jnp.einsum(
        "bqhc,bkhc->bhqk", grad_attn, values, preferred_element_type=jnp.float32
    )
    delta = jnp.sum(
        grad_attn.astype(jnp.float32) * attn_rows.astype(jnp.float32), axis=-1
    ).transpose(0, 2, 1)
    grad_scores = probs * (grad_probs - delta[..., None])
    grad_sb = grad_scores.astype(jnp.bfloat16)
    grad_q = (
        jnp.einsum("bhqk,bkhc->bqhc", grad_sb, key_rows, preferred_element_type=jnp.float32)
        * score_scale
    )
    grad_k = jnp.einsum("bhqk,bqhc->bkhc", grad_sb, queries, preferred_element_type=jnp.float32)
    grad_v = jnp.einsum(
        "bhqk,bqhc->bkhc", probs.astype(jnp.bfloat16), grad_attn, preferred_element_type=jnp.float32
    )
    table_part = jnp.sum(grad_scores, axis=0)
    return (grad_q, grad_k, grad_v, table_part)


def fetch_weights(norm_gains, offsets, qkv_weight, proj_weight, fc1_weight, fc2_weight):
    return (
        lax.all_gather(norm_gains, "dp", axis=0, tiled=True),
        lax.all_gather(offsets, "dp", axis=0, tiled=True),
        lax.all_gather(qkv_weight, "dp", axis=0, tiled=True),
        lax.all_gather(proj_weight, "dp", axis=0, tiled=True),
        lax.all_gather(fc1_weight, "dp", axis=0, tiled=True),
        lax.all_gather(fc2_weight, "dp", axis=0, tiled=True),
    )


def shards(
    block_input,
    out_grad,
    norm_gains,
    offsets,
    qkv_weight,
    qv_bias,
    pos_table,
    proj_weight,
    fc1_weight,
    fc1_bias,
    fc2_weight,
    rel_index,
    region_ids,
):
    win_pos = rel_index.shape[0]
    win_count = TOK_IMG // win_pos
    score_scale = HD ** (-0.5)
    image_count = block_input.shape[0]
    row_count = image_count * TOK_IMG
    heads_here = pos_table.shape[0]
    head_cols = heads_here * HD
    block_size = blocked()
    block_count = image_count // block_size
    win_bias, one_hot = window_terms(pos_table, rel_index, region_ids, block_size)

    def split_heads(flat_rows):
        return flat_rows.reshape(block_count, block_size * win_count, win_pos, heads_here, HD)

    def forward_block(operands):
        return attend(operands[0], operands[1], operands[2], win_bias)

    def backward_block(operands):
        return attend_back(
            operands[0],
            operands[1],
            operands[2],
            operands[3],
            operands[4],
            operands[5],
            win_bias,
            score_scale,
        )

    def gather_all():
        fetched = tuple(
            fetch_weights(norm_gains, offsets, qkv_weight, proj_weight, fc1_weight, fc2_weight)
        )
        return fetched + (qv_bias, fc1_bias)

    gains_w, offsets_w, qkv_w, proj_w, fc1_w, fc2_w, pair_bias, hidden_bias = gather_all()
    gain_cols = gains_w.astype(jnp.float32)
    offset_cols = offsets_w.astype(jnp.float32)
    bias_qv = pair_bias.astype(jnp.float32)
    x_zero = window_order(block_input).reshape(row_count, D).astype(jnp.float32)
    normed1, inv_std1, pre_one = layer_norm(x_zero, gain_cols[:, 0], offset_cols[:, 0])
    h_one = pre_one.astype(jnp.bfloat16)
    qkv_all = jnp.dot(
        h_one, qkv_w.reshape(D, 3 * head_cols), preferred_element_type=jnp.float32
    ).reshape(row_count, 3, head_cols)
    queries = ((qkv_all[:, 0] + bias_qv[0]) * score_scale).astype(jnp.bfloat16)
    key_rows = qkv_all[:, 1].astype(jnp.bfloat16)
    values = (qkv_all[:, 2] + bias_qv[1]).astype(jnp.bfloat16)
    attn_rows, log_total = lax.map(
        forward_block, (split_heads(queries), split_heads(key_rows), split_heads(values))
    )
    attn_flat = attn_rows.reshape(row_count, head_cols)
    attn_out = lax.psum(along_cols(attn_flat, proj_w).astype(jnp.bfloat16), "mp").astype(
        jnp.float32
    )
    x_one = x_zero + attn_out + offset_cols[:, 1]
    normed2, inv_std2, pre_two = layer_norm(x_one, gain_cols[:, 1], offset_cols[:, 2])
    h_two = pre_two.astype(jnp.bfloat16)
    pre_act = jnp.dot(h_two, fc1_w, preferred_element_type=jnp.float32) + hidden_bias.astype(
        jnp.float32
    )
    act_val, act_slope = gelu_parts(pre_act)
    act_rows = act_val.astype(jnp.bfloat16)
    mlp_out = lax.psum(along_cols(act_rows, fc2_w).astype(jnp.bfloat16), "mp").astype(jnp.float32)
    block_rows = (x_one + mlp_out + offset_cols[:, 3]).astype(jnp.bfloat16)
    out_images = grid_order(block_rows.reshape(image_count, TOK_IMG, D))
    gains_w, offsets_w, qkv_w, proj_w, fc1_w, fc2_w, pair_bias, hidden_bias = gather_all()
    gain_cols = gains_w.astype(jnp.float32)
    offset_cols = offsets_w.astype(jnp.float32)
    grad_y = window_order(out_grad).reshape(row_count, D)
    grad_yf = grad_y.astype(jnp.float32)
    grad_fc2b = jnp.sum(grad_yf, axis=0)
    grad_fc2 = along_rows(grad_y, act_rows)
    grad_pre = jnp.dot(grad_y, fc2_w, preferred_element_type=jnp.float32) * act_slope
    grad_preb = grad_pre.astype(jnp.bfloat16)
    grad_fc1 = along_rows(h_two, grad_preb)
    grad_fc1b = jnp.sum(grad_pre, axis=0)
    grad_h2 = lax.psum(along_cols(grad_preb, fc1_w).astype(jnp.bfloat16), "mp").astype(jnp.float32)
    grad_ln2 = jnp.sum(grad_h2 * normed2, axis=0)
    grad_ln2b = jnp.sum(grad_h2, axis=0)
    grad_x1 = grad_yf + norm_back(grad_h2, normed2, inv_std2, gain_cols[:, 1])
    grad_x1b = grad_x1.astype(jnp.bfloat16)
    grad_proj = along_rows(grad_x1b, attn_flat)
    grad_projb = jnp.sum(grad_x1, axis=0)
    grad_attn = jnp.dot(grad_x1b, proj_w, preferred_element_type=jnp.float32).astype(jnp.bfloat16)
    grad_q, grad_k, grad_v, table_part = lax.map(
        backward_block,
        (
            split_heads(queries),
            split_heads(key_rows),
            split_heads(values),
            split_heads(attn_flat),
            split_heads(grad_attn),
            log_total,
        ),
    )
    grad_q = grad_q.reshape(row_count, head_cols)
    grad_k = grad_k.reshape(row_count, head_cols)
    grad_v = grad_v.reshape(row_count, head_cols)
    grad_qv = jnp.stack([jnp.sum(grad_q, axis=0), jnp.sum(grad_v, axis=0)])
    grad_qkv = (
        jnp.stack([grad_q, grad_k, grad_v], axis=1)
        .astype(jnp.bfloat16)
        .reshape(row_count, 3 * head_cols)
    )
    grad_qkvw = along_rows(h_one, grad_qkv).reshape(D, 3, head_cols)
    grad_h1 = lax.psum(
        along_cols(grad_qkv, qkv_w.reshape(D, 3 * head_cols)).astype(jnp.bfloat16), "mp"
    ).astype(jnp.float32)
    grad_ln1 = jnp.sum(grad_h1 * normed1, axis=0)
    grad_ln1b = jnp.sum(grad_h1, axis=0)
    grad_x0 = grad_x1 + norm_back(grad_h1, normed1, inv_std1, gain_cols[:, 0])
    input_share = grid_order(grad_x0.astype(jnp.bfloat16).reshape(image_count, TOK_IMG, D))
    table_grad = jnp.dot(
        jnp.sum(table_part, axis=0).reshape(heads_here, -1),
        one_hot,
        precision=lax.Precision.HIGHEST,
    )
    gains_grad = jnp.stack([grad_ln1, grad_ln2], axis=1)
    offsets_grad = jnp.stack([grad_ln1b, grad_projb, grad_ln2b, grad_fc2b], axis=1)
    grad_qv, table_grad, grad_fc1b = lax.psum((grad_qv, table_grad, grad_fc1b), "dp")
    gains_grad, offsets_grad, grad_qkvw, grad_proj, grad_fc1, grad_fc2 = (
        lax.psum_scatter(
            gains_grad.astype(jnp.bfloat16), "dp", scatter_dimension=0, tiled=True
        ).astype(jnp.float32),
        lax.psum_scatter(
            offsets_grad.astype(jnp.bfloat16), "dp", scatter_dimension=0, tiled=True
        ).astype(jnp.float32),
        lax.psum_scatter(
            grad_qkvw.astype(jnp.bfloat16), "dp", scatter_dimension=0, tiled=True
        ).astype(jnp.float32),
        lax.psum_scatter(
            grad_proj.astype(jnp.bfloat16), "dp", scatter_dimension=0, tiled=True
        ).astype(jnp.float32),
        lax.psum_scatter(
            grad_fc1.astype(jnp.bfloat16), "dp", scatter_dimension=0, tiled=True
        ).astype(jnp.float32),
        lax.psum_scatter(
            grad_fc2.astype(jnp.bfloat16), "dp", scatter_dimension=0, tiled=True
        ).astype(jnp.float32),
    )
    return (
        out_images,
        input_share,
        gains_grad,
        offsets_grad,
        grad_qkvw,
        grad_qv,
        table_grad,
        grad_proj,
        grad_fc1,
        grad_fc1b,
        grad_fc2,
    )


def solution(mesh):
    in_specs = (
        P("dp", None, None),
        P("dp", None, None),
        P("dp", None),
        P("dp", None),
        P("dp", None, "mp"),
        P(None, "mp"),
        P("mp", None),
        P("dp", "mp"),
        P("dp", "mp"),
        P("mp"),
        P("dp", "mp"),
        P(),
        P(),
    )
    out_specs = (
        P("dp", None, None),
        P("dp", None, None),
        P("dp", None),
        P("dp", None),
        P("dp", None, "mp"),
        P(None, "mp"),
        P("mp", None),
        P("dp", "mp"),
        P("dp", "mp"),
        P("mp"),
        P("dp", "mp"),
    )
    return jax.shard_map(shards, mesh=mesh, in_specs=in_specs, out_specs=out_specs, check_vma=False)
```

profile of v0, /device:TPU:0, one launch (start us, length us, event | category | flops | bytes accessed | tf_op | source)
XLA Modules:
  0.0 1215.3 jit_solution(2443523745431153764)
XLA Ops:
  8.6 4.2 slice.119
  12.8 10.3 all-gather
  23.2 8.9 all-gather.1
  32.8 8.6 all_gather.25
  49.9 4.4 copy.104
  54.4 8.4 reshape.269
  62.7 4.6 fusion.91
  72.2 9.7 all_gather.26
  88.5 7.2 reshape.280
  95.8 8.4 copy.112
  104.2 10.7 squeeze.33
  121.1 10.7 squeeze.34
  138.2 21.6 %while.30 = (s32[]{:T(128)}, bf16[2,48,49,4,32]{2,4,3,1,0:T(8,128)(2,1)}, f32[2,48,4,49]{3,2,1,0:T(4,128)S(1)}, bf16[2,48,49,4,32]{2,4,3,1,0:T(8,128)(2,1)}, bf1...) while((s32[]{:T(128)}, ...), condition=%wide.region_5.6_spmd.clone, body=%wide.region_2.5_spmd.clone.sunk | while | flops 63447552 | bytes 31814608 | solution.py:216
  159.8 5.5 copy.114
  165.3 5.8 reshape.249
  171.1 5.0 convolution_convert_fusion.3
  183.5 4.4 copy.116
  187.9 8.4 reshape_reshape.11
  196.4 3.7 convert_bitcast_fusion
  200.1 9.7 copy.101
  209.8 11.5 reshape.259
  221.3 9.9 all_gather.27
  231.2 11.0 all_gather.28
  242.2 109.5 %all-reduce.6.cloned.1.call-done = bf16[4704,512]{1,0:T(8,128)(2,1)} async-done(((bf16[4704,512]{1,0:T(8,128)(2,1)}), bf16[4704,512]{1,0:T(8,128)(2,1)}) %all-reduce.6.cloned.1.call-update) | async-done | bytes 4816912 | tf_op jit(solution)/shard_map/psum | solution.py:220
  351.7 10.0 fusion.98
  361.7 5.5 multiply_reduce_fusion
  370.8 6.7 multiply_convert_fusion
  377.5 9.0 fusion.103
  388.8 4.5 convolution_convert_fusion.1
  393.4 7.4 fusion.80
  400.9 7.4 convolution_convert_fusion.5
  408.3 159.2 %all-reduce.8.cloned.1.call-done = bf16[4704,512]{1,0:T(8,128)(2,1)} async-done(((bf16[4704,512]{1,0:T(8,128)(2,1)}), bf16[4704,512]{1,0:T(8,128)(2,1)}) %all-reduce.8.cloned.1.call-update) | async-done | bytes 4816912 | tf_op jit(solution)/shard_map/psum | solution.py:245
  567.5 10.3 fusion.53
  577.8 8.0 fusion.93
  585.8 3.6 copy-done.5
  591.9 7.3 reshape.272
  599.2 8.7 copy.121
  607.9 42.0 %while.31 = (s32[]{:T(128)}, f32[2,48,49,4,32]{2,4,3,1,0:T(8,128)}, bf16[2,48,49,4,32]{2,4,3,1,0:T(8,128)(2,1)}, f32[2,48,49,4,32]{2,4,3,1,0:T(8,128)}, f32[2,4,...) while((s32[]{:T(128)}, f32[2,48,49,4,32]{2,4,3,1,0:T(8,128)}, ...), condition=%wide.region_16.17_spmd.clone, body=%wide.region_13.16_spmd.clone.sunk | while | flops 153152640 | bytes 111455464 | solution.py:253
  610.6 4.8 fusion.153
  615.5 4.5 fusion.154
  631.7 4.7 fusion.153
  636.5 4.5 fusion.154
  649.9 10.1 copy.137
  660.0 6.6 reshape.273
  666.6 10.1 copy.139
  676.7 6.7 reshape.275
  683.4 7.3 copy.138
  690.8 6.8 reshape.274
  697.5 6.0 fusion.88
  703.6 6.6 fusion.83
  710.3 6.9 convolution_convert_fusion.2
  717.2 4.4 bitcast_convert_fusion
  738.2 14.4 %all-reduce = (f32[2,128]{1,0:T(2,128)}, f32[4,169]{1,0:T(4,128)}, f32[512]{0:T(512)}) all-reduce(f32[2,128]{1,0:T(2,128)S(1)} %pad_maximum_fusion.9, f32[4,169]{1,0:T(4,128)S(1)} %fusion.73, f32[512]{0:T(512)S(1)} %copy-done.48), channel_id=1, replica_groups=mesh['dp'=8,'mp'=4] {'dp'}, use_global_device_ids=true, to_apply=%region_31.32 | all-reduce | flops 1444 | bytes 11552 | tf_op jit(solution)/shard_map/psum | solution.py:288
  754.0 19.0 %reduce-scatter.11.cloned.1.call-done = bf16[64,3,128]{2,0,1:T(8,128)(2,1)} async-done(((bf16[512,3,128]{2,0,1:T(8,128)(2,1)}), bf16[64,3,128]{2,0,1:T(8,128)(2,1)}) %reduce-scatter.11.cloned.1.call-update) | async-done | bytes 49168 | tf_op jit(solution)/shard_map/reduce_scatter | solution.py:296
  774.5 332.8 %all-reduce.10.cloned.1.call-done = (bf16[4704,512]{1,0:T(8,128)(2,1)}, bf16[4704,512]{1,0:T(8,128)(2,1)}) async-done(((bf16[4704,512]{1,0:T(8,128)(2,1)}, bf16[4704,512]{1,0:T(8,128)(2,1)}), (bf16[4704,512]{1,0:T(8,128)(2,1)}, bf16[4704,512]{1,0:T(8,128)(2,1)})) %all-reduce.10.cloned.1.call-update) | async-done | bytes 9633808 | tf_op jit(solution)/shard_map/psum | solution.py:231
  1110.4 10.3 fusion.59
  1121.6 9.2 add_convert_fusion
  1130.8 10.3 fusion.57
  1141.2 8.3 reshape_reshape.10
  1149.5 5.6 copy.115
  1157.3 8.3 reshape_reshape.12
  1165.6 5.6 copy.130
  1174.2 5.7 fusion.67
  1183.9 23.0 %reduce-scatter.21.cloned.1.call-done = bf16[64,4]{1,0:T(8,128)(2,1)} async-done(((bf16[512,4]{1,0:T(8,128)(2,1)}), bf16[64,4]{1,0:T(8,128)(2,1)}) %reduce-scatter.21.cloned.1.call-update) | async-done | bytes 528
  (298 shorter events, 129.1 us)
Async XLA Ops:
  7.2 63.5 %copy-start = (f32[4,169]{1,0:T(4,128)S(1)}, f32[4,169]{1,0:T(4,128)}, u32[]{:S(2)}) copy-start(f32[4,169]{1,0:T(4,128)} %param.23) | copy-start | bytes 8116
  7.2 344.5 %all-reduce.6.cloned.1.call-start = ((), (), s32[]{:S(2)}) async-start(), calls=%async_computation.6 | async-start | bytes 9633792 | tf_op jit(solution)/shard_map/psum | solution.py:220
  7.3 5.5 copy-start.51
  7.3 15.9 %copy-start.49 = (bf16[64,4]{0,1:T(4,128)(2,1)S(1)}, bf16[64,4]{0,1:T(4,128)(2,1)}, u32[]{:S(2)}) copy-start(bf16[64,4]{0,1:T(4,128)(2,1)} %param.20) | copy-start | bytes 1540
  7.3 25.5 %copy-start.37 = (bf16[64,3,128]{2,0,1:T(8,128)(2,1)S(1)}, bf16[64,3,128]{2,0,1:T(8,128)(2,1)}, u32[]{:S(2)}) copy-start(bf16[64,3,128]{2,0,1:T(8,128)(2,1)} %param.21) | copy-start | bytes 147460
  23.2 24.7 %copy-start.38 = (f32[512,1]{0,1:T(1,128)}, f32[512,1]{0,1:T(1,128)S(1)}, u32[]{:S(2)}) copy-start(f32[512,1]{0,1:T(1,128)S(1)} %get-tuple-element.312) | copy-start | bytes 6148
  41.3 3.6 copy-start.23
  68.5 3.8 copy-start.41
  70.5 18.0 %copy-start.42 = (s32[2401]{0:T(1024)}, s32[2401]{0:T(1024)S(1)}, u32[]{:S(2)}) copy-start(s32[2401]{0:T(1024)S(1)} %eq.34) | copy-start | bytes 28816
  81.9 6.6 copy-start.10
  138.4 3.3 copy-start.7
  149.1 3.2 copy-start.7
  176.1 391.4 %all-reduce.8.cloned.1.call-start = ((), (), s32[]{:S(2)}) async-start(), calls=%async_computation.7 | async-start | bytes 9633792 | tf_op jit(solution)/shard_map/psum | solution.py:245
  176.2 3.6 copy-start.50
  209.8 11.5 copy-start.36
  361.7 6.5 copy-start.2
  368.2 9.3 slice-start.6
  370.8 6.7 copy-start.19
  370.8 6.7 slice-start.7
  370.8 6.7 copy-start.30
  393.3 330.6 %reduce-scatter.15.cloned.1.call-start = ((), (), s32[]{:S(2)}) async-start(), calls=%async_computation.10 | async-start | bytes 589824 | tf_op jit(solution)/shard_map/reduce_scatter | solution.py:302
  400.8 324.5 %reduce-scatter.17.cloned.1.call-start = ((), (), s32[]{:S(2)}) async-start(), calls=%async_computation.11 | async-start | bytes 589824 | tf_op jit(solution)/shard_map/reduce_scatter | solution.py:305
  408.3 344.4 %reduce-scatter.13.cloned.1.call-start = ((), (), s32[]{:S(2)}) async-start(), calls=%async_computation.9 | async-start | bytes 147456 | tf_op jit(solution)/shard_map/reduce_scatter | solution.py:299
  585.8 3.6 copy-start.5
  610.6 4.8 copy-start.4
  610.6 4.8 copy-start.9
  610.6 4.8 copy-start.11
  615.4 6.8 slice-start.4
  615.4 4.5 copy-start.33
  615.4 4.6 copy-start.3
  615.4 6.8 slice-start.5
  615.5 8.3 slice-start.2
  620.0 3.7 copy-start.34
  620.0 3.7 slice-start.3
  631.7 4.7 copy-start.4
  631.7 4.7 copy-start.9
  631.7 4.7 copy-start.11
  636.4 6.8 slice-start.4
  636.4 4.5 copy-start.33
  636.4 4.6 copy-start.3
  636.4 6.7 slice-start.5
  636.5 8.3 slice-start.2
  641.0 3.7 copy-start.34
  641.0 3.7 slice-start.3
  676.7 6.7 copy-start.20
  690.7 6.8 copy-start.17
  697.5 6.1 copy-start.25
  703.6 6.7 copy-start.31
  703.6 69.5 %reduce-scatter.11.cloned.1.call-start = ((), (), s32[]{:S(2)}) async-start(), calls=%async_computation.8 | async-start | bytes 442368 | tf_op jit(solution)/shard_map/reduce_scatter | solution.py:296
  710.2 7.0 copy-start.24
  710.2 397.0 %all-reduce.10.cloned.1.call-start = ((), (), s32[]{:S(2)}) async-start(), calls=%async_computation.14 | async-start | bytes 19267584 | tf_op jit(solution)/shard_map/psum | solution.py:231
  710.3 6.9 copy-start.26
  710.3 6.9 copy-start.27
  721.6 460.9 %reduce-scatter.19.cloned.1.call-start = ((), (), s32[]{:S(2)}) async-start(), calls=%async_computation.12 | async-start | bytes 147456
  730.3 6.6 copy-start.35
  730.3 7.0 copy-start.43
  730.3 7.9 copy-start.48
  733.9 376.5 %copy-start.39 = (f32[512,1]{0,1:T(1,128)S(1)}, f32[512,1]{0,1:T(1,128)}, u32[]{:S(2)}) copy-start(f32[512,1]{0,1:T(1,128)} %copy-done.38) | copy-start | bytes 6148
  1110.3 11.3 copy-start.44
  1110.4 20.5 %slice-start = ((s8[4816896]{0:T(1024)(128)(4,1)}), s8[622592]{0:T(1024)(128)(4,1)S(1)}, s32[]{:S(2)}) async-start(s8[4816896]{0:T(1024)(128)(4,1)} %bitcast.240), calls=%async_computation.15 | async-start | bytes 1245184
  1121.6 85.4 %reduce-scatter.21.cloned.1.call-start = ((), (), s32[]{:S(2)}) async-start(), calls=%async_computation.13 | async-start | bytes 147456
  1121.6 9.2 slice-start.1
  1174.2 5.8 copy-start.18
  1174.2 34.1 %copy-start.1 = (f32[4,169]{1,0:T(4,128)S(1)}, f32[4,169]{1,0:T(4,128)}, u32[]{:S(2)}) copy-start(f32[4,169]{1,0:T(4,128)} %param.23) | copy-start | bytes 8116
  (23 other events, 49.9 us)
Sparse Core Ops, SparseCore 0:
  176.2 175.3 all-reduce.5
  393.4 174.0 all-reduce.7
  570.6 33.0 reduce-scatter.14
  606.6 34.1 reduce-scatter.16
  703.7 32.4 reduce-scatter.12
  739.1 33.8 reduce-scatter.10
  776.2 331.0 all-reduce.9
  1121.7 32.5 reduce-scatter.18
  1174.3 32.5 reduce-scatter.20
where the time goes:
time: 1230 us; the launch traced here: 1220 us
  waiting for transfers between devices  644 us (52%)
  local copies, waits for them, and re-layouts  245 us (20%)
  other arithmetic  129 us (10%)
  matrix products  109 us (9%)
  blocking collectives  72.7 us (6%)
  between operations  15.1 us (1%)
    psum x1, waiting for transfers between devices, shards(): lax.psum(along_cols(act_rows, fc2_w).astype(jnp.bfloat16), 'mp')  333 us
    psum x1, waiting for transfers between devices, shards(): lax.psum(along_cols(grad_preb, fc1_w).astype(jnp.bfloat16), 'mp')  159 us
    psum x1, waiting for transfers between devices, shards(): lax.psum(along_cols(attn_flat, proj_w).astype(jnp.bfloat16), 'mp')  109 us
    another operation x6, local copies, waits for them, and re-layouts, shards(): jnp.stack([grad_q, grad_k, grad_v], axis=1).astype(jnp.bfloat16)  47.6 us
    unnamed x101, local copies, waits for them, and re-layouts  35.7 us
    dot_general x4, matrix products, along_rows(): lax.dot_general(left_mat, right_mat, (((0,), (0,)), ((), ())), preferred_...  27.4 us
  transfers between devices with their start and end apart: 9, of which 5 were waited for; matrix products, arithmetic and copies ran while one was open for 23% of the time, Pallas kernels for 0%

commit v1 on v0

--- a/solution.py
+++ b/solution.py
@@ -10,6 +10,12 @@
 SHIFT = 3
 SIDE = 14
 TOK_IMG = 196
+
+
+def gather_and_add(x, axis):
+    shards = lax.all_gather(x, axis, axis=0, tiled=False)
+    total = shards.sum(axis=0)
+    return total
 
 
 def window_order(tokens_in):
@@ -228,7 +234,9 @@
     )
     act_val, act_slope = gelu_parts(pre_act)
     act_rows = act_val.astype(jnp.bfloat16)
-    mlp_out = lax.psum(along_cols(act_rows, fc2_w).astype(jnp.bfloat16), "mp").astype(jnp.float32)
+    mlp_out = gather_and_add(along_cols(act_rows, fc2_w).astype(jnp.bfloat16), "mp").astype(
+        jnp.float32
+    )
     block_rows = (x_one + mlp_out + offset_cols[:, 3]).astype(jnp.bfloat16)
     out_images = grid_order(block_rows.reshape(image_count, TOK_IMG, D))
     gains_w, offsets_w, qkv_w, proj_w, fc1_w, fc2_w, pair_bias, hidden_bias = gather_all()

time: 1230 us -> 1390 us (1.13)
  waiting for transfers between devices: 644 us -> 792 us
    all_gather x0 -> x1, waiting for transfers between devices: none -> 319 us  [gather_and_add(): shards = lax.all_gather(x, axis, axis=0, tiled=False)]
    psum x1, waiting for transfers between devices: 333 us -> 176 us  [shards(): lax.psum(along_cols(grad_qkv, qkv_w.reshape(D, 3 * head_cols)).astype(jnp...]
    reduce_scatter x1, waiting for transfers between devices: 19 us -> 2.11 us  [shards(): lax.psum_scatter(grad_qkvw.astype(jnp.bfloat16), 'dp', scatter_dimension=...]
    unnamed x11 -> x12, waiting for transfers between devices: 23.1 us -> 33.9 us
    unnamed x101 -> x89, local copies, waits for them, and re-layouts: 35.7 us -> 35.8 us
  transfers between devices with their start and end apart: 9 -> 10, of which waited for: 5 -> 6; matrix products, arithmetic and copies ran while one was open for 23% -> 22% of each run, Pallas kernels for 0% -> 0%
where the time goes in v1:
time: 1390 us; the launch traced here: 1380 us
  waiting for transfers between devices  792 us (57%)
  local copies, waits for them, and re-layouts  245 us (18%)
  other arithmetic  140 us (10%)
  matrix products  112 us (8%)
  blocking collectives  72.6 us (5%)
  between operations  15 us (1%)
    all_gather x1, waiting for transfers between devices, gather_and_add(): shards = lax.all_gather(x, axis, axis=0, tiled=False)  319 us
    psum x1, waiting for transfers between devices, shards(): lax.psum(along_cols(grad_qkv, qkv_w.reshape(D, 3 * head_cols)).astype(jnp...  176 us
    psum x1, waiting for transfers between devices, shards(): lax.psum(along_cols(grad_preb, fc1_w).astype(jnp.bfloat16), 'mp')  151 us
    psum x1, waiting for transfers between devices, shards(): lax.psum(along_cols(attn_flat, proj_w).astype(jnp.bfloat16), 'mp')  110 us
    another operation x6, local copies, waits for them, and re-layouts, shards(): jnp.stack([grad_q, grad_k, grad_v], axis=1).astype(jnp.bfloat16)  47.7 us
    unnamed x89, local copies, waits for them, and re-layouts  35.8 us
    unnamed x12, waiting for transfers between devices  33.9 us
  transfers between devices with their start and end apart: 10, of which 6 were waited for; matrix products, arithmetic and copies ran while one was open for 22% of the time, Pallas kernels for 0%

profile of v1, /device:TPU:0, one launch (start us, length us, event | category | flops | bytes accessed | tf_op | source)
XLA Modules:
  0.0 1379.0 jit_solution(2786264535985791960)
XLA Ops:
  8.6 4.2 slice.119
  12.8 10.3 all-gather.1
  23.2 8.9 all-gather.2
  32.8 8.6 all_gather.31
  49.9 4.4 copy.104
  54.3 8.4 reshape.270
  62.7 4.6 fusion.91
  72.2 9.5 all_gather.32
  88.4 7.3 reshape.281
  95.6 8.4 copy.112
  104.0 10.7 squeeze.33
  121.0 10.7 squeeze.34
  138.1 21.8 %while.30 = (s32[]{:T(128)}, bf16[2,48,49,4,32]{2,4,3,1,0:T(8,128)(2,1)}, f32[2,48,4,49]{3,2,1,0:T(4,128)S(1)}, bf16[2,48,49,4,32]{2,4,3,1,0:T(8,128)(2,1)}, bf1...) while((s32[]{:T(128)}, ...), condition=%wide.region_5.6_spmd.clone, body=%wide.region_2.5_spmd.clone.sunk | while | flops 63447552 | bytes 31814608 | solution.py:222
  159.8 5.7 copy.114
  165.5 5.8 reshape.249
  171.3 4.9 convolution_convert_fusion.3
  183.3 4.4 copy.116
  187.7 8.4 reshape_reshape.11
  196.1 3.7 convert_bitcast_fusion
  199.9 9.8 copy.101
  209.7 11.5 reshape.259
  221.2 9.9 all_gather.33
  231.1 11.0 all_gather.34
  242.0 109.7 %all-reduce.5.cloned.1.call-done = bf16[4704,512]{1,0:T(8,128)(2,1)} async-done(((bf16[4704,512]{1,0:T(8,128)(2,1)}), bf16[4704,512]{1,0:T(8,128)(2,1)}) %all-reduce.5.cloned.1.call-update) | async-done | bytes 4816912 | tf_op jit(solution)/shard_map/psum | solution.py:226
  351.7 10.1 fusion.98
  361.8 5.5 multiply_reduce_fusion
  371.0 6.6 multiply_convert_fusion
  377.7 9.0 fusion.103
  388.9 4.5 convolution_convert_fusion.1
  393.4 7.4 convolution_convert_fusion.2
  401.3 7.4 fusion.80
  408.7 7.4 convolution_convert_fusion.5
  416.2 151.3 %all-reduce.7.cloned.1.call-done = bf16[4704,512]{1,0:T(8,128)(2,1)} async-done(((bf16[4704,512]{1,0:T(8,128)(2,1)}), bf16[4704,512]{1,0:T(8,128)(2,1)}) %all-reduce.7.cloned.1.call-update) | async-done | bytes 4816912 | tf_op jit(solution)/shard_map/psum | solution.py:253
  567.6 10.3 fusion.53
  578.5 318.7 %all-gather.5.cloned.1.call-done = bf16[18816,512]{1,0:T(8,128)(2,1)} async-done(((bf16[4704,512]{1,0:T(8,128)(2,1)}), bf16[18816,512]{1,0:T(8,128)(2,1)}) %all-gather.5.cloned.1.call-update) | async-done | bytes 19267600 | tf_op jit(solution)/shard_map/all_gather | solution.py:16
  897.2 13.9 %reduce_sum.205 = bf16[4704,512]{1,0:T(8,128)(2,1)} reduce(bf16[4,4704,512]{2,1,0:T(8,128)(2,1)} %bitcast.254, bf16[]{:T(256)} %constant.64.clone.1), dimensions={0}, to_apply=%region_9.10 | reduce | flops 7225344 | bytes 24084482 | tf_op jit(solution)/shard_map/reduce_sum | solution.py:17
  911.0 11.2 fusion.93
  928.4 7.3 reshape.273
  935.7 8.7 copy.121
  944.4 42.1 %while.31 = (s32[]{:T(128)}, f32[2,48,49,4,32]{2,4,3,1,0:T(8,128)}, bf16[2,48,49,4,32]{2,4,3,1,0:T(8,128)(2,1)}, f32[2,48,49,4,32]{2,4,3,1,0:T(8,128)}, f32[2,4,...) while((s32[]{:T(128)}, f32[2,48,49,4,32]{2,4,3,1,0:T(8,128)}, ...), condition=%wide.region_16.17_spmd.clone, body=%wide.region_13.16_spmd.clone.sunk | while | flops 153152640 | bytes 111455464 | solution.py:261
  947.1 4.7 fusion.153
  951.9 4.5 fusion.154
  968.2 4.7 fusion.153
  973.0 4.5 fusion.154
  986.5 10.1 copy.137
  996.6 6.6 reshape.274
  1003.2 10.1 copy.139
  1013.3 6.9 reshape.276
  1020.2 7.4 copy.138
  1027.5 6.6 reshape.275
  1034.2 6.0 fusion.88
  1040.3 6.6 fusion.83
  1047.0 6.6 bitcast_convert_fusion
  1068.9 8.7 reshape_reshape.10
  1077.7 5.6 copy.115
  1086.8 14.4 %all-reduce = (f32[2,128]{1,0:T(2,128)}, f32[4,169]{1,0:T(4,128)}, f32[512]{0:T(512)}) all-reduce(f32[2,128]{1,0:T(2,128)S(1)} %pad_maximum_fusion.9, f32[4,169]{1,0:T(4,128)S(1)} %fusion.73, f32[512]{0:T(512)S(1)} %copy-done.44), channel_id=1, replica_groups=mesh['dp'=8,'mp'=4] {'dp'}, use_global_device_ids=true, to_apply=%region_31.32 | all-reduce | flops 1444 | bytes 11552 | tf_op jit(solution)/shard_map/psum | solution.py:296
  1101.2 5.1 fusion.67
  1111.2 176.1 %all-reduce.9.cloned.1.call-done = bf16[4704,512]{1,0:T(8,128)(2,1)} async-done(((bf16[4704,512]{1,0:T(8,128)(2,1)}), bf16[4704,512]{1,0:T(8,128)(2,1)}) %all-reduce.9.cloned.1.call-update) | async-done | bytes 4816912 | tf_op jit(solution)/shard_map/psum | solution.py:282
  1290.4 10.2 fusion.59
  1301.5 11.9 fusion.57
  1313.5 8.3 reshape_reshape.12
  1321.8 5.6 copy.130
  1330.4 5.1 fusion.66
  1336.9 33.7 %reduce-scatter.21.cloned.1.call-done = bf16[64,4]{1,0:T(8,128)(2,1)} async-done(((bf16[512,4]{1,0:T(8,128)(2,1)}), bf16[64,4]{1,0:T(8,128)(2,1)}) %reduce-scatter.21.cloned.1.call-update) | async-done | bytes 528
  (288 shorter events, 133.1 us)
Async XLA Ops:
  7.2 63.5 %copy-start = (f32[4,169]{1,0:T(4,128)S(1)}, f32[4,169]{1,0:T(4,128)}, u32[]{:S(2)}) copy-start(f32[4,169]{1,0:T(4,128)} %param.23) | copy-start | bytes 8116
  7.2 344.5 %all-reduce.5.cloned.1.call-start = ((), (), s32[]{:S(2)}) async-start(), calls=%async_computation.6 | async-start | bytes 9633792 | tf_op jit(solution)/shard_map/psum | solution.py:226
  7.3 5.5 copy-start.47
  7.3 15.9 %copy-start.45 = (bf16[64,4]{0,1:T(4,128)(2,1)S(1)}, bf16[64,4]{0,1:T(4,128)(2,1)}, u32[]{:S(2)}) copy-start(bf16[64,4]{0,1:T(4,128)(2,1)} %param.20) | copy-start | bytes 1540
  7.3 25.5 %copy-start.33 = (bf16[64,3,128]{2,0,1:T(8,128)(2,1)S(1)}, bf16[64,3,128]{2,0,1:T(8,128)(2,1)}, u32[]{:S(2)}) copy-start(bf16[64,3,128]{2,0,1:T(8,128)(2,1)} %param.21) | copy-start | bytes 147460
  23.2 24.7 %copy-start.34 = (f32[512,1]{0,1:T(1,128)}, f32[512,1]{0,1:T(1,128)S(1)}, u32[]{:S(2)}) copy-start(f32[512,1]{0,1:T(1,128)S(1)} %get-tuple-element.311) | copy-start | bytes 6148
  41.3 3.6 copy-start.22
  41.5 3.0 copy-start.14
  45.0 2.9 copy-start.6
  68.4 3.8 copy-start.37
  70.5 17.9 %copy-start.38 = (s32[2401]{0:T(1024)}, s32[2401]{0:T(1024)S(1)}, u32[]{:S(2)}) copy-start(s32[2401]{0:T(1024)S(1)} %eq.34) | copy-start | bytes 28816
  81.7 6.7 copy-start.10
  138.6 3.3 copy-start.7
  143.6 2.8 copy-start.12
  149.2 3.3 copy-start.7
  154.2 2.8 copy-start.12
  176.2 391.4 %all-reduce.7.cloned.1.call-start = ((), (), s32[]{:S(2)}) async-start(), calls=%async_computation.7 | async-start | bytes 9633792 | tf_op jit(solution)/shard_map/psum | solution.py:253
  176.2 3.6 copy-start.46
  209.7 11.5 copy-start.32
  361.8 6.5 copy-start.2
  368.3 2.6 copy-start.28
  368.3 9.3 slice-start.4
  371.0 6.7 copy-start.18
  371.0 6.7 slice-start.5
  371.0 6.7 copy-start.27
  393.4 503.8 %all-gather.5.cloned.1.call-start = ((), (), s32[]{:S(2)}) async-start(), calls=%async_computation.13 | async-start | bytes 24084480 | tf_op jit(solution)/shard_map/all_gather | solution.py:16
  400.8 655.1 %reduce-scatter.15.cloned.1.call-start = ((), (), s32[]{:S(2)}) async-start(), calls=%async_computation.11 | async-start | bytes 589824 | tf_op jit(solution)/shard_map/reduce_scatter | solution.py:310
  408.7 648.7 %reduce-scatter.17.cloned.1.call-start = ((), (), s32[]{:S(2)}) async-start(), calls=%async_computation.12 | async-start | bytes 589824 | tf_op jit(solution)/shard_map/reduce_scatter | solution.py:313
  416.2 690.1 %reduce-scatter.13.cloned.1.call-start = ((), (), s32[]{:S(2)}) async-start(), calls=%async_computation.10 | async-start | bytes 147456 | tf_op jit(solution)/shard_map/reduce_scatter | solution.py:307
  897.2 13.9 %copy-start.40 = (f32[512,1]{0,1:T(1,128)S(1)}, f32[512,1]{0,1:T(1,128)}, u32[]{:S(2)}) copy-start(f32[512,1]{0,1:T(1,128)} %get-tuple-element.306) | copy-start | bytes 6148
  922.3 3.7 copy-start.5
  947.1 4.8 copy-start.4
  947.1 4.8 copy-start.9
  947.1 4.8 copy-start.11
  951.8 6.8 slice-start.2
  951.9 4.5 copy-start.29
  951.9 4.6 copy-start.3
  951.9 6.7 slice-start.3
  951.9 8.2 slice-start
  956.5 3.7 copy-start.30
  956.5 3.7 slice-start.1
  960.2 2.6 copy-start.16
  968.1 4.8 copy-start.4
  968.1 4.8 copy-start.9
  968.1 4.8 copy-start.11
  972.9 6.8 slice-start.2
  972.9 4.5 copy-start.29
  972.9 4.6 copy-start.3
  972.9 6.7 slice-start.3
  973.0 8.3 slice-start
  977.5 3.7 copy-start.30
  977.5 3.7 slice-start.1
  981.2 2.6 copy-start.16
  1013.3 6.9 copy-start.19
  1027.5 6.7 copy-start.17
  1034.2 6.1 copy-start.24
  1040.2 6.7 copy-start.23
  1040.2 69.5 %reduce-scatter.11.cloned.1.call-start = ((), (), s32[]{:S(2)}) async-start(), calls=%async_computation.9 | async-start | bytes 442368 | tf_op jit(solution)/shard_map/reduce_scatter | solution.py:304
  1046.9 240.4 %all-reduce.9.cloned.1.call-start = ((), (), s32[]{:S(2)}) async-start(), calls=%async_computation.8 | async-start | bytes 9633792 | tf_op jit(solution)/shard_map/psum | solution.py:282
  1053.7 281.9 %reduce-scatter.19.cloned.1.call-start = ((), (), s32[]{:S(2)}) async-start(), calls=%async_computation.14 | async-start | bytes 147456
  1083.4 3.4 copy-start.44
  1106.3 184.1 %copy-start.35 = (f32[512,1]{0,1:T(1,128)S(1)}, f32[512,1]{0,1:T(1,128)}, u32[]{:S(2)}) copy-start(f32[512,1]{0,1:T(1,128)} %copy-done.34) | copy-start | bytes 6148
  1301.5 69.1 %reduce-scatter.21.cloned.1.call-start = ((), (), s32[]{:S(2)}) async-start(), calls=%async_computation.15 | async-start | bytes 147456
  1330.4 41.6 %copy-start.1 = (f32[4,169]{1,0:T(4,128)S(1)}, f32[4,169]{1,0:T(4,128)}, u32[]{:S(2)}) copy-start(f32[4,169]{1,0:T(4,128)} %param.23) | copy-start | bytes 8116
  (18 other events, 35.2 us)
Sparse Core Ops, SparseCore 0:
  176.3 175.3 all-reduce.4
  393.5 174.0 all-reduce.6
  569.2 327.9 all-gather.4
  900.1 32.8 reduce-scatter.14
  936.0 34.1 reduce-scatter.16
  1040.4 32.3 reduce-scatter.12
  1075.8 33.8 reduce-scatter.10
  1112.1 175.1 all-reduce.8
  1301.6 32.4 reduce-scatter.18
  1337.0 33.5 reduce-scatter.20
